TPU v7x, 32 devices: a whole 2x2x4 slice. The times are simulated.
32 devices in a mesh: groups: 2 (over x), seq: 8 (over z, y), head: 2 (over core).
Axes of the slice: x: 2, y: 2, z: 4, core: 2. Of those that a mesh axis runs over, the one named last changes fastest.
Arguments:
- queries: bfloat16 [2048, 28, 128], P(('groups', 'seq'), 'head'), parts along dimension 0, may hold values from -400 to 400, as said below
- request_image: int32 [2048, 1], P(('groups', 'seq')), parts along dimension 0, may hold values from 0 to 15; in each aligned block of 128 rows (0 to 127, 128 to 255, ...) at most 16 rows name the same one
- image_slot: int32 [32], P('groups'), parts along dimension 0, may hold values from 0 to 15, each once
- image_lengths: int32 [32], P(('groups', 'seq')), parts along dimension 0, may hold values from 640 to 1280
- image_keys: bfloat16 [32, 4, 1280, 128], P(('groups', 'seq'), 'head'), parts along dimension 0, may hold values from -6 to 6
- image_values: bfloat16 [32, 4, 1280, 128], P(('groups', 'seq'), 'head'), parts along dimension 0, may hold values from -6 to 6
- text_keys: bfloat16 [2048, 4, 64, 128], P(('groups', 'seq'), 'head'), parts along dimension 0, may hold values from -6 to 6
- text_values: bfloat16 [2048, 4, 64, 128], P(('groups', 'seq'), 'head'), parts along dimension 0, may hold values from -6 to 6
- text_lengths: int32 [2048], P(('groups', 'seq')), parts along dimension 0, may hold values from 1 to 64
Outputs:
- attention: bfloat16 [2048, 28, 128], P(('groups', 'seq'), 'head'), parts along dimension 0
There are 2 independent parts, one for each index of `groups`. A program takes and returns all parts, laid end to end along the dimension named above; each array names one. Nothing has to cross between parts.
Inputs may be any that keep to these rules, and one draw needn't show every extreme that they name: queries are finite bfloat16 values. `request_image`: the requests of one index of seq name any one image at most 16 times, and in some index of seq some image is named exactly 16 times. `image_slot`: a permutation; the image in storage slot s is held by index s // 2 of seq.
All inputs are finite; a program needn't handle non-finite values.
Results may differ from a plain program's by a relative error of at most 0.0056.
Values may be sent and summed in bfloat16 or wider, within the bound.
No kernel may reach another device: no remote copies, remote signals or barrier semaphores. Data moves between devices by JAX's collectives and lax.ppermute only.
A program may use at most 64 MiB of HBM per device.

v0:
```python
import math

import jax
import jax.numpy as jnp
from jax import lax
from jax.sharding import PartitionSpec as P

NEGATIVE = -1e30


def weigh(scores, valid):
    scores = jnp.where(valid, scores, NEGATIVE)
    highest = jnp.max(scores, axis=-1, keepdims=True)
    weights = jnp.where(valid, jnp.exp(scores - highest), 0.0)
    total = jnp.sum(weights, axis=-1, keepdims=True)
    return (weights.astype(jnp.bfloat16), total, highest)


def on_device(
    queries,
    request_image,
    image_slot,
    image_lengths,
    image_keys,
    image_values,
    text_keys,
    text_values,
    text_lengths,
):
    rows, local_heads, head_size = queries.shape
    local_kv = image_keys.shape[1]
    group = local_heads // local_kv
    images = image_slot.shape[0]
    held = image_keys.shape[0]
    image_tokens = image_keys.shape[2]
    text_tokens = text_keys.shape[2]
    devices = lax.axis_size("seq")
    most = max(2, 2 * rows // images)
    width = local_heads * head_size
    scale = 1.0 / math.sqrt(head_size)
    image_ids = jnp.arange(images, dtype=jnp.int32)
    chosen = request_image == image_ids[None, :]
    slots = jnp.sum(jnp.where(chosen, image_slot[None, :], 0), axis=1)
    slot_hits = (slots[:, None] == image_ids[None, :]).astype(jnp.int32)
    ranks = jnp.sum(slot_hits * (jnp.cumsum(slot_hits, axis=0) - 1), axis=1)
    targets = slots * most + ranks
    dispatch = (jnp.arange(images * most, dtype=jnp.int32)[:, None] == targets[None, :]).astype(
        jnp.bfloat16
    )
    flat_queries = queries.reshape(rows, width)
    outgoing = jnp.dot(dispatch, flat_queries, preferred_element_type=jnp.float32).astype(
        jnp.bfloat16
    )
    outgoing = outgoing.reshape(devices, held, most, width)
    incoming = lax.all_to_all(outgoing, "seq", split_axis=0, concat_axis=0, tiled=True)
    sources = incoming.shape[0]
    count = incoming.shape[2]
    outputs = []
    sums = []
    for index in range(held):
        heads = incoming[:, index].reshape(sources * count, local_kv, group, head_size)
        scores = (
            jnp.einsum(
                "rhgd,htd->rhgt", heads, image_keys[index], preferred_element_type=jnp.float32
            )
            * scale
        )
        valid = jnp.arange(image_tokens, dtype=jnp.int32) < image_lengths[index]
        weights, total, highest = weigh(scores, valid)
        output = (
            jnp.einsum(
                "rhgt,htd->rhgd", weights, image_values[index], preferred_element_type=jnp.float32
            )
            / total
        )
        lse_value = highest[..., 0] + jnp.log(total[..., 0])
        outputs.append(output.astype(jnp.bfloat16).reshape(sources, count, width))
        sums.append(lse_value.reshape(sources, count, local_heads))
    stacked_out = jnp.stack(outputs, axis=1)
    stacked_lse = jnp.stack(sums, axis=1)
    back_out = lax.all_to_all(stacked_out, "seq", split_axis=0, concat_axis=0, tiled=True)
    back_lse = lax.all_to_all(stacked_lse, "seq", split_axis=0, concat_axis=0, tiled=True)
    flat_back = back_out.reshape(images * most, width)
    image_part = jnp.einsum("sr,sc->rc", dispatch, flat_back, preferred_element_type=jnp.float32)
    image_part = image_part.reshape(rows, local_kv, group, head_size)
    image_lse = jnp.einsum(
        "sr,sc->rc",
        dispatch.astype(jnp.float32),
        back_lse.reshape(images * most, local_heads),
        precision=lax.Precision.HIGHEST,
    )
    image_lse = image_lse.reshape(rows, local_kv, group)
    heads = queries.reshape(rows, local_kv, group, head_size)
    scores = (
        jnp.einsum("rhgd,rhtd->rhgt", heads, text_keys, preferred_element_type=jnp.float32) * scale
    )
    valid = (jnp.arange(text_tokens, dtype=jnp.int32)[None, :] < text_lengths[:, None])[
        :, None, None, :
    ]
    weights, total, highest = weigh(scores, valid)
    text_out = (
        jnp.einsum("rhgt,rhtd->rhgd", weights, text_values, preferred_element_type=jnp.float32)
        / total
    )
    text_lse = highest[..., 0] + jnp.log(total[..., 0])
    upper = jnp.maximum(image_lse, text_lse)
    image_weight = jnp.exp(image_lse - upper)[..., None]
    text_weight = jnp.exp(text_lse - upper)[..., None]
    merged = (image_weight * image_part + text_weight * text_out) / (image_weight + text_weight)
    return merged.reshape(rows, local_heads, head_size).astype(jnp.bfloat16)


def solution(mesh):
    in_specs = (
        P(("groups", "seq"), "head", None),
        P(("groups", "seq"), None),
        P("groups"),
        P(("groups", "seq")),
        P(("groups", "seq"), "head", None, None),
        P(("groups", "seq"), "head", None, None),
        P(("groups", "seq"), "head", None, None),
        P(("groups", "seq"), "head", None, None),
        P(("groups", "seq")),
    )
    out_specs = P(("groups", "seq"), "head", None)
    return jax.shard_map(
        on_device, mesh=mesh, in_specs=in_specs, out_specs=out_specs, check_vma=False
    )
```

profile of v0, /device:TPU:0, one launch (start us, length us, event | category | flops | bytes accessed | tf_op | source)
XLA Modules:
  0.0 91.5 jit_solution(16366865769194857306)
XLA Ops:
  0.0 1.3 %copy.55 = bf16[128,14,128]{0,2,1:T(8,128)(2,1)S(1)} copy(bf16[128,14,128]{2,0,1:T(8,128)(2,1)} %param.9) | data formatting | bytes 917504 | tf_op args[0]
  1.3 0.8 select_reduce_fusion.1
  2.6 1.4 %convolution_convert_fusion = bf16[256,1792]{1,0:T(8,128)(2,1)} fusion(bf16[128,1792]{0,1:T(8,128)(2,1)S(1)} %bitcast.119, s32[128]{0:T(128)S(1)} %multiply_add_fusion), kind=kOutput, calls=%fused_computation.20 | convolution fusion | flops 117964800 | bytes 1376768 | tf_op jit(solution)/shard_map/dot_general | solution.py:51
  4.0 7.3 %all-to-all-start = ((bf16[8,2,16,1792]{3,2,1,0:T(8,128)(2,1)}), bf16[8,2,16,1792]{3,2,1,0:T(8,128)(2,1)S(1)}, u32[]{:S(2)}, u32[]{:S(2)}) async-start(bf16[8,2,16,1792]{3,2,1,0:T(8,128)(2,1)} %bitcast.4), calls=%async_computation | async-start | bytes 1835008 | tf_op jit(solution)/shard_map/all_to_all | solution.py:55
  11.3 1.3 %fusion.83 = (s32[1]{0:T(128)}, s32[1]{0:T(128)}) fusion(s32[2]{0:T(128)} %param.12), kind=kLoop, calls=%fused_computation.90 | loop fusion | bytes 16 | tf_op jit(solution)/shard_map/slice | solution.py:68
  12.7 0.6 iota_compare_fusion.4
  13.3 0.7 iota_compare_fusion.5
  14.0 20.4 %all-to-all-done = bf16[8,2,16,1792]{3,2,1,0:T(8,128)(2,1)S(1)} async-done(((bf16[8,2,16,1792]{3,2,1,0:T(8,128)(2,1)}), bf16[8,2,16,1792]{3,2,1,0:T(8,128)(2,1)S(1)}, u32[]{:S(2)}, u32[]{:S(2)}) %all-to-all-start) | async-done | bytes 917536 | tf_op jit(solution)/shard_map/all_to_all | solution.py:55
  34.4 0.5 reshape_squeeze.7
  35.0 2.9 %bitcast_reduce_fusion = (f32[128,2,7]{0,2,1:T(8,128)S(1)}, f32[2,128,7,1280]{3,1,2,0:T(8,128)S(1)}) fusion(pred[1280]{0:T(1024)(128)(4,1)S(1)} %iota_compare_fusion.4, bf16[2,2,1280,128]{3,2,1,0:T(8,128)(2,1)} %param.13, bf16[128,2,7,128]{3,2,1,0:T(8,128)(2,1)S(1)} %reshape_squeeze.7), kind=kOutput, calls=%fused_computation.1 | convolution fusion | flops 594082048 | bytes 10297600 | tf_op jit(solution)/shard_map/rhgd,htd->rhgt/dot_general | solution.py:63
  37.9 2.4 %fusion.7 = f32[128,2,7]{0,2,1:T(8,128)S(1)} fusion(f32[2,128,7,1280]{3,1,2,0:T(8,128)S(1)} %get-tuple-element.13, f32[128,2,7]{0,2,1:T(8,128)S(1)} %get-tuple-element.12, pred[1280]{0:T(1024)(128)(4,1)S(1)} %iota_compare_fusion.4), kind=kLoop, calls=%fused_computation.13 | loop fusion | flops 11467008 | bytes 9190656 | tf_op jit(solution)/shard_map/reduce_sum | solution.py:15
  40.4 2.2 %fusion.29 = bf16[128,2,7,128]{3,0,2,1:T(8,128)(2,1)S(1)} fusion(f32[2,128,7,1280]{3,1,2,0:T(8,128)S(1)} %get-tuple-element.13, f32[128,2,7]{0,2,1:T(8,128)S(1)} %get-tuple-element.12, pred[1280]{0:T(1024)(128)(4,1)S(1)} %iota_compare_fusion.4, bf16[2,2,1280,128]{3,2,1,0:T(8,128)(2,1)S(1)} %copy-done.3, f32[128,2,7]{0,2,1:T(8,128)S(1)} %fusion.7), kind=kOutput, calls=%fused_computation.31 | convolution fusion | flops 599130112 | bytes 10309632 | tf_op jit(solution)/shard_map/rhgt,htd->rhgd/dot_general | solution.py:71
  42.6 0.5 reshape_squeeze.6
  43.2 1.8 %bitcast_reduce_fusion.1 = (f32[128,2,7]{0,2,1:T(8,128)S(1)}, f32[2,128,7,1280]{3,1,2,0:T(8,128)S(1)}) fusion(pred[1280]{0:T(1024)(128)(4,1)S(1)} %iota_compare_fusion.5, bf16[2,2,1280,128]{3,2,1,0:T(8,128)(2,1)S(1)} %copy-done.1, bf16[128,2,7,128]{3,2,1,0:T(8,128)(2,1)S(1)} %reshape_squeeze.6), kind=kOutput, calls=%fused_computation.5 | convolution fusion | flops 594082048 | bytes 10363904 | tf_op jit(solution)/shard_map/rhgd,htd->rhgt/dot_general | solution.py:63
  44.9 2.4 %fusion.5 = f32[128,2,7]{0,2,1:T(8,128)S(1)} fusion(f32[2,128,7,1280]{3,1,2,0:T(8,128)S(1)} %get-tuple-element.15, f32[128,2,7]{0,2,1:T(8,128)S(1)} %get-tuple-element.14, pred[1280]{0:T(1024)(128)(4,1)S(1)} %iota_compare_fusion.5), kind=kLoop, calls=%fused_computation.11 | loop fusion | flops 11467008 | bytes 9190656 | tf_op jit(solution)/shard_map/reduce_sum | solution.py:15
  47.4 2.2 %fusion.35 = bf16[128,2,7,128]{3,0,2,1:T(8,128)(2,1)S(1)} fusion(f32[2,128,7,1280]{3,1,2,0:T(8,128)S(1)} %get-tuple-element.15, f32[128,2,7]{0,2,1:T(8,128)S(1)} %get-tuple-element.14, pred[1280]{0:T(1024)(128)(4,1)S(1)} %iota_compare_fusion.5, bf16[2,2,1280,128]{3,2,1,0:T(8,128)(2,1)S(1)} %copy-done.4, f32[128,2,7]{0,2,1:T(8,128)S(1)} %fusion.5), kind=kOutput, calls=%fused_computation.33 | convolution fusion | flops 599130112 | bytes 10309632 | tf_op jit(solution)/shard_map/rhgt,htd->rhgd/dot_general | solution.py:71
  49.7 0.3 copy.65
  50.0 0.5 stack_reshape.9
  50.8 0.5 stack_reshape.8
  51.6 0.8 reshape.111
  52.3 3.5 %all-to-all-start.1 = ((f32[8,1,448]{2,1,0:T(1,128)}), f32[8,1,448]{2,1,0:T(1,128)S(1)}, u32[]{:S(2)}, u32[]{:S(2)}) async-start(f32[8,1,448]{2,1,0:T(1,128)} %reshape.111), calls=%async_computation.1 | async-start | bytes 32768 | tf_op jit(solution)/shard_map/all_to_all | solution.py:82
  56.0 1.0 %copy.66 = bf16[8,2,16,1792]{3,2,1,0:T(8,128)(2,1)} copy(bf16[8,2,16,1792]{3,2,0,1:T(8,128)(2,1)S(1)} %pad_maximum_fusion) | data formatting | bytes 1835008 | tf_op jit(solution)/shard_map/stack | solution.py:79
  57.0 5.4 %all-to-all-done.1 = f32[8,1,448]{2,1,0:T(1,128)S(1)} async-done(((f32[8,1,448]{2,1,0:T(1,128)}), f32[8,1,448]{2,1,0:T(1,128)S(1)}, u32[]{:S(2)}, u32[]{:S(2)}) %all-to-all-start.1) | async-done | bytes 14368 | tf_op jit(solution)/shard_map/all_to_all | solution.py:82
  62.4 3.7 %all-to-all-start.2 = ((bf16[8,2,16,1792]{3,2,1,0:T(8,128)(2,1)}), bf16[8,2,16,1792]{3,2,1,0:T(8,128)(2,1)S(1)}, u32[]{:S(2)}, u32[]{:S(2)}) async-start(bf16[8,2,16,1792]{3,2,1,0:T(8,128)(2,1)} %copy.66), calls=%async_computation.2 | async-start | bytes 1835008 | tf_op jit(solution)/shard_map/all_to_all | solution.py:81
  66.3 4.6 %fusion.84 = (f32[128,2,7]{2,1,0:T(2,128)S(1)}, f32[128,2,7,64]{3,2,1,0:T(8,128)S(1)}) fusion(bf16[128,2,64,128]{3,2,1,0:T(8,128)(2,1)} %param.15, bf16[128,2,7,128]{3,0,2,1:T(8,128)(2,1)S(1)} %bitcast.118, pred[128,64]{1,0:T(8,128)(4,1)S(1)} %iota_compare_fusion.1), kind=kOutput, calls=%fused_computation.91 | convolution fusion | flops 29702400 | bytes 5127168 | tf_op jit(solution)/shard_map/rhgd,rhtd->rhgt/dot_general | solution.py:95
  71.0 0.8 fusion.40
  71.9 4.5 %fusion.51 = f32[128,2,7,128]{3,2,1,0:T(8,128)} fusion(bf16[128,2,64,128]{3,2,1,0:T(8,128)(2,1)} %param.16, f32[128,2,7,64]{3,2,1,0:T(8,128)S(1)} %get-tuple-element.17, f32[128,2,7]{2,1,0:T(2,128)S(1)} %get-tuple-element.16, pred[128,64]{1,0:T(8,128)(4,1)S(1)} %iota_compare_fusion.1), kind=kOutput, calls=%fused_computation.49 | convolution fusion | flops 29704192 | bytes 5585920 | tf_op jit(solution)/shard_map/rhgt,rhtd->rhgd/dot_general | solution.py:102
  76.4 0.5 broadcast.62
  76.9 0.7 reduce
  78.2 9.7 %all-to-all-done.2 = bf16[8,2,16,1792]{3,2,1,0:T(8,128)(2,1)S(1)} async-done(((bf16[8,2,16,1792]{3,2,1,0:T(8,128)(2,1)}), bf16[8,2,16,1792]{3,2,1,0:T(8,128)(2,1)S(1)}, u32[]{:S(2)}, u32[]{:S(2)}) %all-to-all-start.2) | async-done | bytes 917536 | tf_op jit(solution)/shard_map/all_to_all | solution.py:81
  87.9 0.5 copy.67
  88.5 3.0 %fusion.25 = bf16[128,2,7,128]{3,0,2,1:T(8,128)(2,1)} fusion(bf16[2,7,128,256]{3,2,1,0:T(8,128)(2,1)S(1)} %bitcast.120, f32[128,2,7,128]{3,2,1,0:T(8,128)} %fusion.51, f32[128,2,7]{0,2,1:T(8,128)S(1)} %get-tuple-element.5, f32[128,2,7]{0,2,1:T(8,128)S(1)} %copy.62, f32[128,2,7]{0,2,1:T(8,128)S(1)} %get-tuple-element.6, ...), kind=kOutput, calls=%fused_computation.28 | convolution fusion | flops 118849536 | bytes 2322944 | tf_op jit(solution)/shard_map/sr,sc->rc/dot_general | solution.py:84
  (31 shorter events, 2.0 us)
Async XLA Ops:
  4.0 30.3 %all-to-all-start = ((bf16[8,2,16,1792]{3,2,1,0:T(8,128)(2,1)}), bf16[8,2,16,1792]{3,2,1,0:T(8,128)(2,1)S(1)}, u32[]{:S(2)}, u32[]{:S(2)}) async-start(bf16[8,2,16,1792]{3,2,1,0:T(8,128)(2,1)} %bitcast.4), calls=%async_computation | async-start | bytes 1835008 | tf_op jit(solution)/shard_map/all_to_all | solution.py:55
  35.0 5.4 %copy-start.3 = (bf16[2,2,1280,128]{3,2,1,0:T(8,128)(2,1)S(1)}, bf16[2,2,1280,128]{3,2,1,0:T(8,128)(2,1)}, u32[]{:S(2)}) copy-start(bf16[2,2,1280,128]{3,2,1,0:T(8,128)(2,1)} %param.14) | copy-start | bytes 3932164
  40.4 2.8 %copy-start.1 = (bf16[2,2,1280,128]{3,2,1,0:T(8,128)(2,1)S(1)}, bf16[2,2,1280,128]{3,2,1,0:T(8,128)(2,1)}, u32[]{:S(2)}) copy-start(bf16[2,2,1280,128]{3,2,1,0:T(8,128)(2,1)} %param.13) | copy-start | bytes 3932164
  43.2 4.2 %copy-start.4 = (bf16[2,2,1280,128]{3,2,1,0:T(8,128)(2,1)S(1)}, bf16[2,2,1280,128]{3,2,1,0:T(8,128)(2,1)}, u32[]{:S(2)}) copy-start(bf16[2,2,1280,128]{3,2,1,0:T(8,128)(2,1)} %param.14) | copy-start | bytes 3932164
  49.6 16.6 %copy-start.2 = (s32[128]{0:T(128)S(1)}, s32[128]{0:T(128)}, u32[]{:S(2)}) copy-start(s32[128]{0:T(128)} %param.17) | copy-start | bytes 1540
  49.6 16.7 %copy-start = (bf16[128,14,128]{2,0,1:T(8,128)(2,1)S(1)}, bf16[128,14,128]{2,0,1:T(8,128)(2,1)}, u32[]{:S(2)}) copy-start(bf16[128,14,128]{2,0,1:T(8,128)(2,1)} %param.9) | copy-start | bytes 1376260
  52.3 10.1 %all-to-all-start.1 = ((f32[8,1,448]{2,1,0:T(1,128)}), f32[8,1,448]{2,1,0:T(1,128)S(1)}, u32[]{:S(2)}, u32[]{:S(2)}) async-start(f32[8,1,448]{2,1,0:T(1,128)} %reshape.111), calls=%async_computation.1 | async-start | bytes 32768 | tf_op jit(solution)/shard_map/all_to_all | solution.py:82
  62.4 25.5 %all-to-all-start.2 = ((bf16[8,2,16,1792]{3,2,1,0:T(8,128)(2,1)}), bf16[8,2,16,1792]{3,2,1,0:T(8,128)(2,1)S(1)}, u32[]{:S(2)}, u32[]{:S(2)}) async-start(bf16[8,2,16,1792]{3,2,1,0:T(8,128)(2,1)} %copy.66), calls=%async_computation.2 | async-start | bytes 1835008 | tf_op jit(solution)/shard_map/all_to_all | solution.py:81
where the time goes:
time: 92 us; the launch traced here: 91.5 us
  waiting for transfers between devices  35.5 us (39%)
  matrix products  23 us (25%)
  starting transfers between devices  14.6 us (16%)
  other arithmetic  9.09 us (10%)
  local copies, waits for them, and re-layouts  8.97 us (10%)
    all_to_all x1, waiting for transfers between devices, on_device(): lax.all_to_all(outgoing, 'seq', split_axis=0, concat_axis=0, tiled=True)  20.4 us
    all_to_all x1, waiting for transfers between devices, on_device(): lax.all_to_all(stacked_out, 'seq', split_axis=0, concat_axis=0, tiled=True)  9.69 us
    all_to_all x1, starting transfers between devices, on_device(): lax.all_to_all(outgoing, 'seq', split_axis=0, concat_axis=0, tiled=True)  7.31 us
    reduce_sum x3, other arithmetic, weigh(): total = jnp.sum(weights, axis=-1, keepdims=True)  5.66 us
    all_to_all x1, waiting for transfers between devices, on_device(): lax.all_to_all(stacked_lse, 'seq', split_axis=0, concat_axis=0, tiled=True)  5.45 us
    dot_general x2, matrix products, on_device(): jnp.einsum('rhgd,htd->rhgt', heads, image_keys[index], preferred_element_...  4.69 us
    dot_general x1, matrix products, on_device(): jnp.einsum('rhgd,rhtd->rhgt', heads, text_keys, preferred_element_type=jn...  4.62 us
    dot_general x2, matrix products, on_device(): jnp.einsum('rhgt,htd->rhgd', weights, image_values[index], preferred_elem...  4.48 us
  transfers between devices with their start and end apart: 3, of which 3 were waited for; matrix products, arithmetic and copies ran while one was open for 17% of the time, Pallas kernels for 0%

commit v1 on v0

--- a/solution.py
+++ b/solution.py
@@ -1,8 +1,11 @@
+import functools
 import math
 
 import jax
 import jax.numpy as jnp
 from jax import lax
+from jax.experimental import pallas as pl
+from jax.experimental.pallas import tpu as pltpu
 from jax.sharding import PartitionSpec as P
 
 NEGATIVE = -1e30
@@ -14,6 +17,88 @@
     weights = jnp.where(valid, jnp.exp(scores - highest), 0.0)
     total = jnp.sum(weights, axis=-1, keepdims=True)
     return (weights.astype(jnp.bfloat16), total, highest)
+
+LANES = 128
+PIECES = 3
+
+
+def image_body(lengths, queries, keys, values, out, *, group, scale):
+    sources, count, _ = queries.shape
+    local_kv, tokens, head_size = keys.shape
+    rows = sources * count
+    index = pl.program_id(0)
+    length = lengths[index]
+    factor = scale * math.log2(math.e)
+    valid = lax.broadcasted_iota(jnp.int32, (tokens, head_size), 0) < length
+    lane = lax.broadcasted_iota(jnp.int32, (rows, LANES), 1)
+    local_heads = local_kv * group
+    lse_all = jnp.zeros((rows, LANES), jnp.float32)
+    ones = jnp.where(valid, 1.0, 0.0).astype(jnp.bfloat16)
+    for kv in range(local_kv):
+        kept = keys[kv].astype(jnp.float32)
+        kept = jnp.where(valid, kept, kept[0:1]).astype(jnp.bfloat16)
+        value = jnp.where(valid, values[kv].astype(jnp.float32), 0.0).astype(jnp.bfloat16)
+        value = jnp.concatenate([value, ones], axis=1)
+        start = 0
+        while start < group:
+            take = 2 if group - start != 3 else 3
+            take = min(take, group - start)
+            heads = [kv * group + start + j for j in range(take)]
+            block = jnp.concatenate(
+                [
+                    queries[:, :, h * head_size : (h + 1) * head_size].reshape(rows, head_size)
+                    for h in heads
+                ],
+                axis=0,
+            )
+            scores = lax.dot_general(
+                block, kept, (((1,), (1,)), ((), ())), preferred_element_type=jnp.float32
+            )
+            highest = jnp.max(scores, axis=1, keepdims=True)
+            weights = jnp.exp2((scores - highest) * factor).astype(jnp.bfloat16)
+            summed = jnp.dot(weights, value, preferred_element_type=jnp.float32)
+            total = summed[:, head_size:]
+            result = (summed[:, :head_size] / total).astype(jnp.bfloat16)
+            lse = highest * scale + jnp.log(total)
+            for j, h in enumerate(heads):
+                out[:, :, h * head_size : (h + 1) * head_size] = result[
+                    j * rows : (j + 1) * rows
+                ].reshape(sources, count, head_size)
+                lse_all = jnp.where(lane % local_heads == h, lse[j * rows : (j + 1) * rows], lse_all)
+            start += take
+    high = lse_all.astype(jnp.bfloat16).astype(jnp.float32)
+    middle = (lse_all - high).astype(jnp.bfloat16).astype(jnp.float32)
+    low = lse_all - high - middle
+    piece = jnp.where(lane < local_heads, high, jnp.where(lane < 2 * local_heads, middle, low))
+    width = local_heads * head_size
+    out[:, :, width : width + LANES] = piece.astype(jnp.bfloat16).reshape(sources, count, LANES)
+
+
+def attend_images(incoming, image_keys, image_values, image_lengths, group, scale):
+    sources, held, count, width = incoming.shape
+    if count % 16:
+        incoming = incoming.transpose(1, 0, 2, 3).reshape(1, held, sources * count, width)
+    lead, _, inner, _ = incoming.shape
+    _, local_kv, tokens, head_size = image_keys.shape
+    wide = width + LANES
+    cache = pl.BlockSpec((None, local_kv, tokens, head_size), lambda i: (i, 0, 0, 0))
+    out = pl.pallas_call(
+        functools.partial(image_body, group=group, scale=scale),
+        grid=(held,),
+        in_specs=[
+            pl.BlockSpec(memory_space=pltpu.SMEM),
+            pl.BlockSpec((lead, None, inner, width), lambda i: (0, i, 0, 0)),
+            cache,
+            cache,
+        ],
+        out_specs=pl.BlockSpec((lead, None, inner, wide), lambda i: (0, i, 0, 0)),
+        out_shape=jax.ShapeDtypeStruct((lead, held, inner, wide), jnp.bfloat16),
+        compiler_params=pltpu.CompilerParams(vmem_limit_bytes=48 * 1024 * 1024),
+        name="image_attention",
+    )(image_lengths, incoming, image_keys, image_values)
+    if count % 16:
+        out = out.reshape(held, sources, count, wide).transpose(1, 0, 2, 3)
+    return out
 
 
 def on_device(
@@ -53,42 +138,13 @@
     )
     outgoing = outgoing.reshape(devices, held, most, width)
     incoming = lax.all_to_all(outgoing, "seq", split_axis=0, concat_axis=0, tiled=True)
-    sources = incoming.shape[0]
-    count = incoming.shape[2]
-    outputs = []
-    sums = []
-    for index in range(held):
-        heads = incoming[:, index].reshape(sources * count, local_kv, group, head_size)
-        scores = (
-            jnp.einsum(
-                "rhgd,htd->rhgt", heads, image_keys[index], preferred_element_type=jnp.float32
-            )
-            * scale
-        )
-        valid = jnp.arange(image_tokens, dtype=jnp.int32) < image_lengths[index]
-        weights, total, highest = weigh(scores, valid)
-        output = (
-            jnp.einsum(
-                "rhgt,htd->rhgd", weights, image_values[index], preferred_element_type=jnp.float32
-            )
-            / total
-        )
-        lse_value = highest[..., 0] + jnp.log(total[..., 0])
-        outputs.append(output.astype(jnp.bfloat16).reshape(sources, count, width))
-        sums.append(lse_value.reshape(sources, count, local_heads))
-    stacked_out = jnp.stack(outputs, axis=1)
-    stacked_lse = jnp.stack(sums, axis=1)
-    back_out = lax.all_to_all(stacked_out, "seq", split_axis=0, concat_axis=0, tiled=True)
-    back_lse = lax.all_to_all(stacked_lse, "seq", split_axis=0, concat_axis=0, tiled=True)
-    flat_back = back_out.reshape(images * most, width)
-    image_part = jnp.einsum("sr,sc->rc", dispatch, flat_back, preferred_element_type=jnp.float32)
-    image_part = image_part.reshape(rows, local_kv, group, head_size)
-    image_lse = jnp.einsum(
-        "sr,sc->rc",
-        dispatch.astype(jnp.float32),
-        back_lse.reshape(images * most, local_heads),
-        precision=lax.Precision.HIGHEST,
-    )
+    stacked = attend_images(incoming, image_keys, image_values, image_lengths, group, scale)
+    back = lax.all_to_all(stacked, "seq", split_axis=0, concat_axis=0, tiled=True)
+    flat_back = back.reshape(images * most, width + LANES)
+    fetched = jnp.einsum("sr,sc->rc", dispatch, flat_back, preferred_element_type=jnp.float32)
+    image_part = fetched[:, :width].reshape(rows, local_kv, group, head_size)
+    pieces = fetched[:, width : width + PIECES * local_heads]
+    image_lse = jnp.sum(pieces.reshape(rows, PIECES, local_heads), axis=1)
     image_lse = image_lse.reshape(rows, local_kv, group)
     heads = queries.reshape(rows, local_kv, group, head_size)
     scores = (

time: 92 us -> 77.5 us (0.84)
  blocking collectives: 0 us -> 30.5 us
  waiting for transfers between devices: 35.5 us -> 18.4 us
  matrix products: 23 us -> 8.67 us
  starting transfers between devices: 14.6 us -> 3.55 us
  Pallas kernels: 0 us -> 8.86 us
  other arithmetic: 9.09 us -> 2.37 us
  local copies, waits for them, and re-layouts: 8.97 us -> 4.69 us
    all_to_all x0 -> x1, blocking collectives: none -> 30.5 us  [on_device(): lax.all_to_all(outgoing, 'seq', split_axis=0, concat_axis=0, tiled=True)]
    all_to_all x3 -> x1, waiting for transfers between devices: 35.5 us -> 18.4 us  [on_device(): lax.all_to_all(stacked, 'seq', split_axis=0, concat_axis=0, tiled=True)]
    all_to_all x3 -> x1, starting transfers between devices: 14.6 us -> 3.55 us  [on_device(): lax.all_to_all(stacked, 'seq', split_axis=0, concat_axis=0, tiled=True)]
    dot_general x5 -> x0, matrix products: 9.44 us -> none  [the longest x2 4.69 us: on_device(): jnp.einsum('rhgd,htd->rhgt', heads, image_keys[index], preferred_element_...]
    pallas_call x0 -> x1, Pallas kernels: none -> 8.86 us  [attend_images(): pl.pallas_call(functools.partial(image_body, group=group, scale=scale), g...]
    reduce_sum x3 -> x1, other arithmetic: 5.66 us -> 0.83 us  [weigh(): total = jnp.sum(weights, axis=-1, keepdims=True)]
    another operation x6 -> x0, local copies, waits for them, and re-layouts: 3.17 us -> none  [the longest x3 2.05 us: on_device(): stacked_out = jnp.stack(outputs, axis=1)]
    dot_general x1, matrix products: 3.03 us -> 0.35 us  [on_device(): jnp.einsum('sr,sc->rc', dispatch, flat_back, preferred_element_type=jnp.f...]
  transfers between devices with their start and end apart: 3 -> 1, of which waited for: 3 -> 1; matrix products, arithmetic and copies ran while one was open for 17% -> 7% of each run, Pallas kernels for 0% -> 0%
where the time goes in v1:
time: 77.5 us; the launch traced here: 77.2 us
  blocking collectives  30.5 us (39%)
  waiting for transfers between devices  18.4 us (24%)
  Pallas kernels  8.86 us (11%)
  matrix products  8.67 us (11%)
  local copies, waits for them, and re-layouts  4.69 us (6%)
  starting transfers between devices  3.55 us (5%)
  other arithmetic  2.37 us (3%)
    all_to_all x1, blocking collectives, on_device(): lax.all_to_all(outgoing, 'seq', split_axis=0, concat_axis=0, tiled=True)  30.5 us
    all_to_all x1, waiting for transfers between devices, on_device(): lax.all_to_all(stacked, 'seq', split_axis=0, concat_axis=0, tiled=True)  18.4 us
    pallas_call x1, Pallas kernels, attend_images(): pl.pallas_call(functools.partial(image_body, group=group, scale=scale), g...  8.86 us
    dot_general x1, matrix products, on_device(): jnp.einsum('rhgd,rhtd->rhgt', heads, text_keys, preferred_element_type=jn...  4.64 us
    all_to_all x1, starting transfers between devices, on_device(): lax.all_to_all(stacked, 'seq', split_axis=0, concat_axis=0, tiled=True)  3.55 us
    dot_general x1, matrix products, on_device(): jnp.einsum('rhgt,rhtd->rhgd', weights, text_values, preferred_element_typ...  3.26 us
  transfers between devices with their start and end apart: 1, of which 1 were waited for; matrix products, arithmetic and copies ran while one was open for 7% of the time, Pallas kernels for 0%

profile of v1, /device:TPU:0, one launch (start us, length us, event | category | flops | bytes accessed | tf_op | source)
XLA Modules:
  0.0 77.2 jit_solution(10331435561909018789)
XLA Ops:
  0.0 1.0 %select_reduce_fusion.1 = s32[128]{0:T(128)S(1)} fusion(s32[16]{0:T(128)} %param.11, s32[128]{0:T(128)} %bitcast.20), kind=kLoop, calls=%fused_computation.23 | loop fusion | flops 6016 | bytes 1088 | tf_op jit(solution)/shard_map/reduce_sum | solution.py:128
  1.0 0.1 fusion.15
  1.1 0.2 reduce_window_sum.11
  1.3 0.2 select_reduce_fusion
  1.5 1.3 %copy.31 = bf16[128,14,128]{0,2,1:T(8,128)(2,1)S(1)} copy(bf16[128,14,128]{2,0,1:T(8,128)(2,1)} %param.9) | data formatting | bytes 917504 | tf_op args[0]
  2.8 0.4 convolution_convert_fusion
  3.2 0.0 copy-start.4
  3.2 0.0 copy-start.3
  3.2 30.5 %all_to_all.10.queries = bf16[8,2,16,1792]{3,2,1,0:T(8,128)(2,1)S(1)} all-to-all(bf16[8,2,16,1792]{3,2,1,0:T(8,128)(2,1)S(1)} %bitcast.16), channel_id=1, replica_groups=mesh['groups'=2,'seq'=8,'head'=2] {'seq'}, dimensions={0} | all-to-all | bytes 1835008 | tf_op jit(solution)/shard_map/all_to_all | solution.py:140
  33.7 0.0 copy-done.1
  33.7 0.0 copy-done
  33.8 0.0 copy-done.2
  33.8 8.9 %image_attention.1 = bf16[8,2,16,1920]{3,2,1,0:T(8,128)(2,1)} custom-call(s32[2]{0:T(128)S(1)} %copy-done.2, bf16[8,2,16,1792]{3,2,1,0:T(8,128)(2,1)S(1)} %all_to_all.10.queries, bf16[2,2,1280,128]{3,2,1,0:T(8,128)(2,1)S(1)} %copy-done, bf16[2,2,1280,128]{3,2,1,0:T(8,128)(2,1)S(1)} %copy-done.1), custom_call_target="tpu_custom_call" | custom-call | tf_op jit(solution)/shard_map/image_attention/pallas_call | solution.py:85
  42.6 3.6 %all-to-all-start.1 = ((bf16[8,2,16,1920]{3,2,1,0:T(8,128)(2,1)}), bf16[8,2,16,1920]{3,2,1,0:T(8,128)(2,1)S(1)}, u32[]{:S(2)}, u32[]{:S(2)}) async-start(bf16[8,2,16,1920]{3,2,1,0:T(8,128)(2,1)} %image_attention.1), calls=%async_computation.1 | async-start | bytes 1966080 | tf_op jit(solution)/shard_map/all_to_all | solution.py:142
  46.2 0.0 copy-done.4
  46.2 0.1 iota_compare_fusion.3
  46.3 0.0 copy-done.3
  46.3 4.6 %fusion.22 = (f32[128,2,7]{2,1,0:T(2,128)S(1)}, f32[128,2,7,64]{3,2,1,0:T(8,128)S(1)}) fusion(bf16[128,2,64,128]{3,2,1,0:T(8,128)(2,1)} %param.15, bf16[128,2,7,128]{3,0,2,1:T(8,128)(2,1)S(1)} %bitcast.18, pred[128,64]{1,0:T(8,128)(4,1)S(1)} %iota_compare_fusion.3), kind=kOutput, calls=%fused_computation.33 | convolution fusion | flops 29702400 | bytes 5127168 | tf_op jit(solution)/shard_map/rhgd,rhtd->rhgt/dot_general | solution.py:151
  50.9 0.1 copy.35
  51.0 0.8 %fusion.6 = f32[128,2,7]{2,1,0:T(2,128)S(1)} fusion(f32[128,2,7,64]{3,2,1,0:T(8,128)S(1)} %get-tuple-element.9, f32[128,2,7]{2,1,0:T(2,128)S(1)} %get-tuple-element.8, pred[128,64]{1,0:T(8,128)(4,1)S(1)} %iota_compare_fusion.3), kind=kLoop, calls=%fused_computation.10 | loop fusion | flops 342272 | bytes 481280 | tf_op jit(solution)/shard_map/reduce_sum | solution.py:18
  51.8 0.1 copy.34
  51.9 18.4 %all-to-all-done.1 = bf16[8,2,16,1920]{3,2,1,0:T(8,128)(2,1)S(1)} async-done(((bf16[8,2,16,1920]{3,2,1,0:T(8,128)(2,1)}), bf16[8,2,16,1920]{3,2,1,0:T(8,128)(2,1)S(1)}, u32[]{:S(2)}, u32[]{:S(2)}) %all-to-all-start.1) | async-done | bytes 983072 | tf_op jit(solution)/shard_map/all_to_all | solution.py:142
  70.3 0.4 fusion.12
  70.7 0.1 slice.9
  70.7 0.1 copy.32
  70.9 0.3 copy.39
  71.1 1.4 %copy.40 = f32[128,2,7,128]{3,2,1,0:T(8,128)} copy(f32[128,2,7,128]{0,3,2,1:T(8,128)S(1)} %bitcast.17) | data formatting | bytes 1835008 | tf_op jit(solution)/shard_map/reshape | solution.py:145
  72.6 0.2 copy.42
  72.8 0.2 copy.41
  72.9 0.2 copy.38
  73.1 3.3 %fusion.4 = bf16[128,2,7,128]{3,2,1,0:T(8,128)(2,1)S(1)} fusion(bf16[128,2,64,128]{3,2,1,0:T(8,128)(2,1)} %param.16, f32[128,2,7,128]{3,2,1,0:T(8,128)} %copy.40, f32[128,2,7,64]{3,2,1,0:T(8,128)S(1)} %get-tuple-element.9, f32[128,2,7]{2,1,0:T(2,128)S(1)} %copy.42, f32[128,2,7]{2,1,0:T(2,128)S(1)} %fusion.6, f32[128,2,7]{2,1,0:T(2,128)S(1)} %copy.41, ...), kind=kOutput, calls=%fused_computation.7 | convolution fusion | flops 31080448 | bytes 6073344 | tf_op jit(solution)/shard_map/rhgt,rhtd->rhgd/dot_general | solution.py:158
  76.3 0.9 %copy.43 = bf16[128,2,7,128]{3,0,2,1:T(8,128)(2,1)} copy(bf16[128,2,7,128]{3,2,1,0:T(8,128)(2,1)S(1)} %fusion.4) | data formatting | bytes 917504 | tf_op jit(solution)/shard_map/convert_element_type | solution.py:166
  (9 shorter events, 0.1 us)
Async XLA Ops:
  0.0 33.7 %copy-start.1 = (bf16[2,2,1280,128]{3,2,1,0:T(8,128)(2,1)S(1)}, bf16[2,2,1280,128]{3,2,1,0:T(8,128)(2,1)}, u32[]{:S(2)}) copy-start(bf16[2,2,1280,128]{3,2,1,0:T(8,128)(2,1)} %values.1) | copy-start | bytes 3932164
  0.0 33.7 %copy-start = (bf16[2,2,1280,128]{3,2,1,0:T(8,128)(2,1)S(1)}, bf16[2,2,1280,128]{3,2,1,0:T(8,128)(2,1)}, u32[]{:S(2)}) copy-start(bf16[2,2,1280,128]{3,2,1,0:T(8,128)(2,1)} %keys.1) | copy-start | bytes 3932164
  0.0 33.7 %copy-start.2 = (s32[2]{0:T(128)S(1)}, s32[2]{0:T(128)}, u32[]{:S(2)}) copy-start(s32[2]{0:T(128)} %lengths.1) | copy-start | bytes 28
  3.2 43.0 %copy-start.4 = (s32[128]{0:T(128)S(1)}, s32[128]{0:T(128)}, u32[]{:S(2)}) copy-start(s32[128]{0:T(128)} %param.17) | copy-start | bytes 1540
  3.2 43.1 %copy-start.3 = (bf16[128,14,128]{2,0,1:T(8,128)(2,1)S(1)}, bf16[128,14,128]{2,0,1:T(8,128)(2,1)}, u32[]{:S(2)}) copy-start(bf16[128,14,128]{2,0,1:T(8,128)(2,1)} %param.9) | copy-start | bytes 1376260
  42.6 27.7 %all-to-all-start.1 = ((bf16[8,2,16,1920]{3,2,1,0:T(8,128)(2,1)}), bf16[8,2,16,1920]{3,2,1,0:T(8,128)(2,1)S(1)}, u32[]{:S(2)}, u32[]{:S(2)}) async-start(bf16[8,2,16,1920]{3,2,1,0:T(8,128)(2,1)} %image_attention.1), calls=%async_computation.1 | async-start | bytes 1966080 | tf_op jit(solution)/shard_map/all_to_all | solution.py:142

commit v2 on v1

--- a/solution.py
+++ b/solution.py
@@ -101,6 +101,84 @@
     return out
 
 
+def prepare_body(request_image, image_slot, queries, outgoing, targets, *, most):
+    local_heads, rows, _ = queries.shape
+    images = image_slot.shape[1]
+    ids = lax.broadcasted_iota(jnp.int32, (rows, images), 1)
+    slot_values = jnp.where(request_image[...] == ids, image_slot[...], 0).astype(jnp.float32)
+    slots = jnp.sum(slot_values, axis=1, keepdims=True)
+    hits = jnp.where(ids.astype(jnp.float32) == slots, 1.0, 0.0)
+    earlier = lax.broadcasted_iota(jnp.int32, (rows, rows), 1) < lax.broadcasted_iota(
+        jnp.int32, (rows, rows), 0
+    )
+    before = jnp.dot(
+        jnp.where(earlier, 1.0, 0.0).astype(jnp.bfloat16),
+        hits.astype(jnp.bfloat16),
+        preferred_element_type=jnp.float32,
+    )
+    ranks = jnp.sum(hits * before, axis=1, keepdims=True)
+    places = (slots * most + ranks).astype(jnp.int32)
+    targets[...] = places
+    columns = lax.broadcasted_iota(jnp.int32, (rows, images * most), 1)
+    dispatch = jnp.where(columns == places, 1.0, 0.0).astype(jnp.bfloat16)
+    flat = jnp.concatenate([queries[h] for h in range(local_heads)], axis=1)
+    outgoing[...] = lax.dot_general(
+        dispatch, flat, (((0,), (0,)), ((), ())), preferred_element_type=jnp.float32
+    ).astype(jnp.bfloat16)
+
+
+def prepare(request_image, image_slot, queries, most):
+    rows, local_heads, head_size = queries.shape
+    images = image_slot.shape[0]
+    return pl.pallas_call(
+        functools.partial(prepare_body, most=most),
+        out_shape=(
+            jax.ShapeDtypeStruct((images * most, local_heads * head_size), jnp.bfloat16),
+            jax.ShapeDtypeStruct((rows, 1), jnp.int32),
+        ),
+        compiler_params=pltpu.CompilerParams(vmem_limit_bytes=16 * 1024 * 1024),
+        name="prepare",
+    )(request_image, image_slot.reshape(1, images), queries.transpose(1, 0, 2))
+
+
+def merge_body(targets, back, text, text_lse, out):
+    local_heads, rows, head_size = out.shape
+    places = back.shape[0]
+    width = local_heads * head_size
+    columns = lax.broadcasted_iota(jnp.int32, (rows, places), 1)
+    dispatch = jnp.where(columns == targets[...], 1.0, 0.0).astype(jnp.bfloat16)
+    pieces = jnp.dot(dispatch, back[:, width:], preferred_element_type=jnp.float32)
+    source = lax.broadcasted_iota(jnp.int32, (LANES, LANES), 0)
+    target = lax.broadcasted_iota(jnp.int32, (LANES, LANES), 1)
+    joined = (source == target) & (target < local_heads)
+    for piece in range(1, PIECES):
+        joined = joined | ((source == target + piece * local_heads) & (target < local_heads))
+    image_lse = jnp.dot(
+        pieces.astype(jnp.bfloat16),
+        jnp.where(joined, 1.0, 0.0).astype(jnp.bfloat16),
+        preferred_element_type=jnp.float32,
+    )[:, :local_heads]
+    upper = jnp.maximum(image_lse, text_lse[...])
+    image_weight = jnp.exp(image_lse - upper)
+    share = image_weight / (image_weight + jnp.exp(text_lse[...] - upper))
+    image = jnp.dot(dispatch, back[:, :width], preferred_element_type=jnp.float32)
+    for h in range(local_heads):
+        own = text[h]
+        part = image[:, h * head_size : (h + 1) * head_size]
+        out[h] = (own + share[:, h : h + 1] * (part - own)).astype(jnp.bfloat16)
+
+
+def merge(targets, back, text, text_lse, local_heads):
+    rows = targets.shape[0]
+    head_size = text.shape[2]
+    return pl.pallas_call(
+        merge_body,
+        out_shape=jax.ShapeDtypeStruct((local_heads, rows, head_size), jnp.bfloat16),
+        compiler_params=pltpu.CompilerParams(vmem_limit_bytes=16 * 1024 * 1024),
+        name="merge",
+    )(targets, back, text, text_lse).transpose(1, 0, 2)
+
+
 def on_device(
     queries,
     request_image,
@@ -123,29 +201,12 @@
     most = max(2, 2 * rows // images)
     width = local_heads * head_size
     scale = 1.0 / math.sqrt(head_size)
-    image_ids = jnp.arange(images, dtype=jnp.int32)
-    chosen = request_image == image_ids[None, :]
-    slots = jnp.sum(jnp.where(chosen, image_slot[None, :], 0), axis=1)
-    slot_hits = (slots[:, None] == image_ids[None, :]).astype(jnp.int32)
-    ranks = jnp.sum(slot_hits * (jnp.cumsum(slot_hits, axis=0) - 1), axis=1)
-    targets = slots * most + ranks
-    dispatch = (jnp.arange(images * most, dtype=jnp.int32)[:, None] == targets[None, :]).astype(
-        jnp.bfloat16
-    )
-    flat_queries = queries.reshape(rows, width)
-    outgoing = jnp.dot(dispatch, flat_queries, preferred_element_type=jnp.float32).astype(
-        jnp.bfloat16
-    )
+    outgoing, targets = prepare(request_image, image_slot, queries, most)
     outgoing = outgoing.reshape(devices, held, most, width)
     incoming = lax.all_to_all(outgoing, "seq", split_axis=0, concat_axis=0, tiled=True)
     stacked = attend_images(incoming, image_keys, image_values, image_lengths, group, scale)
     back = lax.all_to_all(stacked, "seq", split_axis=0, concat_axis=0, tiled=True)
     flat_back = back.reshape(images * most, width + LANES)
-    fetched = jnp.einsum("sr,sc->rc", dispatch, flat_back, preferred_element_type=jnp.float32)
-    image_part = fetched[:, :width].reshape(rows, local_kv, group, head_size)
-    pieces = fetched[:, width : width + PIECES * local_heads]
-    image_lse = jnp.sum(pieces.reshape(rows, PIECES, local_heads), axis=1)
-    image_lse = image_lse.reshape(rows, local_kv, group)
     heads = queries.reshape(rows, local_kv, group, head_size)
     scores = (
         jnp.einsum("rhgd,rhtd->rhgt", heads, text_keys, preferred_element_type=jnp.float32) * scale
@@ -159,11 +220,8 @@
         / total
     )
     text_lse = highest[..., 0] + jnp.log(total[..., 0])
-    upper = jnp.maximum(image_lse, text_lse)
-    image_weight = jnp.exp(image_lse - upper)[..., None]
-    text_weight = jnp.exp(text_lse - upper)[..., None]
-    merged = (image_weight * image_part + text_weight * text_out) / (image_weight + text_weight)
-    return merged.reshape(rows, local_heads, head_size).astype(jnp.bfloat16)
+    text_flat = text_out.reshape(rows, local_heads, head_size).transpose(1, 0, 2)
+    return merge(targets, flat_back, text_flat, text_lse.reshape(rows, local_heads), local_heads)
 
 
 def solution(mesh):

time: 77.5 us -> 75.4 us (0.973)
  waiting for transfers between devices: 18.4 us -> 14.4 us
  Pallas kernels: 8.86 us -> 11.1 us
  local copies, waits for them, and re-layouts: 4.69 us -> 6.3 us
  other arithmetic: 2.37 us -> 0.92 us
    unnamed x11 -> x15, local copies, waits for them, and re-layouts: 1.32 us -> 5.73 us
    all_to_all x1, waiting for transfers between devices: 18.4 us -> 14.4 us  [on_device(): lax.all_to_all(stacked, 'seq', split_axis=0, concat_axis=0, tiled=True)]
    pallas_call x0 -> x2, Pallas kernels: none -> 2.28 us  [the longest x1 1.49 us: merge(): pl.pallas_call(merge_body, out_shape=jax.ShapeDtypeStruct((local_heads, r...]
    reshape x3 -> x0, local copies, waits for them, and re-layouts: 1.43 us -> none  [the longest x1 1.41 us: on_device(): image_part = fetched[:, :width].reshape(rows, local_kv, group, head_size)]
    reduce_sum x3 -> x0, other arithmetic: 1.17 us -> none  [the longest x1 0.99 us: on_device(): slots = jnp.sum(jnp.where(chosen, image_slot[None, :], 0), axis=1)]
    convert_element_type x1 -> x0, local copies, waits for them, and re-layouts: 0.9 us -> none  [on_device(): return merged.reshape(rows, local_heads, head_size).astype(jnp.bfloat16)]
  transfers between devices with their start and end apart: 1 -> 1, of which waited for: 1 -> 1; matrix products, arithmetic and copies ran while one was open for 7% -> 13% of each run, Pallas kernels for 0% -> 0%
where the time goes in v2:
time: 75.4 us; the launch traced here: 75 us
  blocking collectives  30.5 us (40%)
  waiting for transfers between devices  14.4 us (19%)
  Pallas kernels  11.1 us (15%)
  matrix products  8.08 us (11%)
  local copies, waits for them, and re-layouts  6.3 us (8%)
  starting transfers between devices  3.55 us (5%)
  other arithmetic  0.92 us (1%)
    all_to_all x1, blocking collectives, on_device(): lax.all_to_all(outgoing, 'seq', split_axis=0, concat_axis=0, tiled=True)  30.5 us
    all_to_all x1, waiting for transfers between devices, on_device(): lax.all_to_all(stacked, 'seq', split_axis=0, concat_axis=0, tiled=True)  14.4 us
    pallas_call x1, Pallas kernels, attend_images(): pl.pallas_call(functools.partial(image_body, group=group, scale=scale), g...  8.8 us
    unnamed x15, local copies, waits for them, and re-layouts  5.73 us
    dot_general x1, matrix products, on_device(): jnp.einsum('rhgd,rhtd->rhgt', heads, text_keys, preferred_element_type=jn...  4.62 us
    all_to_all x1, starting transfers between devices, on_device(): lax.all_to_all(stacked, 'seq', split_axis=0, concat_axis=0, tiled=True)  3.55 us
    dot_general x1, matrix products, on_device(): jnp.einsum('rhgt,rhtd->rhgd', weights, text_values, preferred_element_typ...  3.46 us
  transfers between devices with their start and end apart: 1, of which 1 were waited for; matrix products, arithmetic and copies ran while one was open for 13% of the time, Pallas kernels for 0%

profile of v2, /device:TPU:0, one launch (start us, length us, event | category | flops | bytes accessed | tf_op | source)
XLA Modules:
  0.0 75.0 jit_solution(3034225453644443129)
XLA Ops:
  0.0 0.8 %copy.24.request_image = s32[128,1]{1,0:T(8,128)S(1)} copy(s32[128,1]{0,1:T(1,128)} %param.10) | data formatting | bytes 1024 | tf_op args[1]
  0.8 0.0 copy-start
  0.8 1.0 %copy-done = bf16[128,14,128]{2,0,1:T(8,128)(2,1)S(1)} copy-done((bf16[128,14,128]{2,0,1:T(8,128)(2,1)S(1)}, bf16[128,14,128]{2,0,1:T(8,128)(2,1)}, u32[]{:S(2)}) %copy-start) | copy-done | bytes 458776
  1.8 0.0 copy-start.4
  1.8 0.7 copy-done.4
  2.4 0.8 %prepare.1 = (bf16[256,1792]{1,0:T(8,128)(2,1)S(1)}, s32[128,1]{1,0:T(8,128)S(1)}) custom-call(s32[128,1]{1,0:T(8,128)S(1)} %copy.24.request_image, s32[1,16]{1,0:T(1,128)S(1)} %bitcast.18, bf16[14,128,128]{2,1,0:T(8,128)(2,1)S(1)} %bitcast.15), custom_call_target="tpu_custom_call" | custom-call | tf_op jit(solution)/shard_map/prepare/pallas_call | solution.py:133
  3.2 0.0 copy-start.6
  3.2 0.0 copy-start.1
  3.3 30.5 %all_to_all.10.queries = bf16[8,2,16,1792]{3,2,1,0:T(8,128)(2,1)S(1)} all-to-all(bf16[8,2,16,1792]{3,2,1,0:T(8,128)(2,1)S(1)} %bitcast.17), channel_id=1, replica_groups=mesh['groups'=2,'seq'=8,'head'=2] {'seq'}, dimensions={0} | all-to-all | bytes 1835008 | tf_op jit(solution)/shard_map/all_to_all | solution.py:206
  33.8 0.0 copy-start.2
  33.8 1.3 %copy-done.2 = bf16[2,2,1280,128]{3,2,1,0:T(8,128)(2,1)S(1)} copy-done((bf16[2,2,1280,128]{3,2,1,0:T(8,128)(2,1)S(1)}, bf16[2,2,1280,128]{3,2,1,0:T(8,128)(2,1)}, u32[]{:S(2)}) %copy-start.2) | copy-done | bytes 1310744
  35.1 0.0 copy-start.3
  35.1 1.3 %copy-done.3 = bf16[2,2,1280,128]{3,2,1,0:T(8,128)(2,1)S(1)} copy-done((bf16[2,2,1280,128]{3,2,1,0:T(8,128)(2,1)S(1)}, bf16[2,2,1280,128]{3,2,1,0:T(8,128)(2,1)}, u32[]{:S(2)}) %copy-start.3) | copy-done | bytes 1310744
  36.4 0.0 copy-start.5
  36.4 0.7 copy-done.5
  37.1 8.8 %image_attention.1 = bf16[8,2,16,1920]{3,2,1,0:T(8,128)(2,1)} custom-call(s32[2]{0:T(128)S(1)} %copy-done.5, bf16[8,2,16,1792]{3,2,1,0:T(8,128)(2,1)S(1)} %all_to_all.10.queries, bf16[2,2,1280,128]{3,2,1,0:T(8,128)(2,1)S(1)} %copy-done.2, bf16[2,2,1280,128]{3,2,1,0:T(8,128)(2,1)S(1)} %copy-done.3), custom_call_target="tpu_custom_call" | custom-call | tf_op jit(solution)/shard_map/image_attention/pallas_call | solution.py:85
  45.9 3.6 %all-to-all-start.1 = ((bf16[8,2,16,1920]{3,2,1,0:T(8,128)(2,1)}), bf16[8,2,16,1920]{3,2,1,0:T(8,128)(2,1)S(1)}, u32[]{:S(2)}, u32[]{:S(2)}) async-start(bf16[8,2,16,1920]{3,2,1,0:T(8,128)(2,1)} %image_attention.1), calls=%async_computation.1 | async-start | bytes 1966080 | tf_op jit(solution)/shard_map/all_to_all | solution.py:208
  49.4 0.0 copy-done.6
  49.4 0.1 iota_compare_fusion
  49.5 0.0 copy-done.1
  49.5 4.6 %fusion.9 = (f32[128,2,7]{2,1,0:T(2,128)S(1)}, f32[128,2,7,64]{3,2,1,0:T(8,128)S(1)}) fusion(bf16[128,2,64,128]{3,2,1,0:T(8,128)(2,1)} %param.15, bf16[128,2,7,128]{3,0,2,1:T(8,128)(2,1)S(1)} %bitcast.16, pred[128,64]{1,0:T(8,128)(4,1)S(1)} %iota_compare_fusion), kind=kOutput, calls=%fused_computation.13 | convolution fusion | flops 29702400 | bytes 5127168 | tf_op jit(solution)/shard_map/rhgd,rhtd->rhgt/dot_general | solution.py:212
  54.2 0.1 copy.28
  54.3 0.8 %fusion.1 = f32[128,2,7]{2,1,0:T(2,128)S(1)} fusion(f32[128,2,7,64]{3,2,1,0:T(8,128)S(1)} %get-tuple-element.10, f32[128,2,7]{2,1,0:T(2,128)S(1)} %get-tuple-element.9, pred[128,64]{1,0:T(8,128)(4,1)S(1)} %iota_compare_fusion), kind=kLoop, calls=%fused_computation.4 | loop fusion | flops 342272 | bytes 481280 | tf_op jit(solution)/shard_map/reduce_sum | solution.py:18
  55.1 0.1 copy.27
  55.2 3.5 %convolution_divide_fusion = f32[128,2,7,128]{3,2,1,0:T(8,128)S(1)} fusion(bf16[128,2,64,128]{3,2,1,0:T(8,128)(2,1)} %param.16, f32[128,2,7,64]{3,2,1,0:T(8,128)S(1)} %get-tuple-element.10, f32[128,2,7]{2,1,0:T(2,128)S(1)} %fusion.1, f32[128,2,7]{2,1,0:T(2,128)S(1)} %get-tuple-element.9, pred[128,64]{1,0:T(8,128)(4,1)S(1)} %iota_compare_fusion), kind=kOutput, calls=%fused_computation | convolution fusion | flops 29933568 | bytes 5593088 | tf_op jit(solution)/shard_map/rhgt,rhtd->rhgd/dot_general | solution.py:219
  58.6 0.3 copy.26
  59.0 0.1 copy.30.text_lse
  59.1 14.4 %all-to-all-done.1 = bf16[8,2,16,1920]{3,2,1,0:T(8,128)(2,1)S(1)} async-done(((bf16[8,2,16,1920]{3,2,1,0:T(8,128)(2,1)}), bf16[8,2,16,1920]{3,2,1,0:T(8,128)(2,1)S(1)}, u32[]{:S(2)}, u32[]{:S(2)}) %all-to-all-start.1) | async-done | bytes 983072 | tf_op jit(solution)/shard_map/all_to_all | solution.py:208
  73.5 1.5 %merge.1 = bf16[14,128,128]{2,1,0:T(8,128)(2,1)} custom-call(s32[128,1]{1,0:T(8,128)S(1)} %get-tuple-element.7.targets, bf16[256,1920]{1,0:T(8,128)(2,1)S(1)} %bitcast.13, f32[14,128,128]{2,1,0:T(8,128)S(1)} %bitcast.14, f32[128,14]{1,0:T(8,128)S(1)} %copy.30.text_lse), custom_call_target="tpu_custom_call" | custom-call | tf_op jit(solution)/shard_map/merge/pallas_call | solution.py:174
  (3 shorter events, 0.0 us)
Async XLA Ops:
  0.8 1.0 %copy-start = (bf16[128,14,128]{2,0,1:T(8,128)(2,1)S(1)}, bf16[128,14,128]{2,0,1:T(8,128)(2,1)}, u32[]{:S(2)}) copy-start(bf16[128,14,128]{2,0,1:T(8,128)(2,1)} %param.9) | copy-start | bytes 1376260
  1.8 0.7 copy-start.4
  3.2 46.2 %copy-start.6 = (s32[128]{0:T(128)S(1)}, s32[128]{0:T(128)}, u32[]{:S(2)}) copy-start(s32[128]{0:T(128)} %param.17) | copy-start | bytes 1540
  3.2 46.3 %copy-start.1 = (bf16[128,14,128]{2,0,1:T(8,128)(2,1)S(1)}, bf16[128,14,128]{2,0,1:T(8,128)(2,1)}, u32[]{:S(2)}) copy-start(bf16[128,14,128]{2,0,1:T(8,128)(2,1)} %param.9) | copy-start | bytes 1376260
  33.8 1.3 %copy-start.2 = (bf16[2,2,1280,128]{3,2,1,0:T(8,128)(2,1)S(1)}, bf16[2,2,1280,128]{3,2,1,0:T(8,128)(2,1)}, u32[]{:S(2)}) copy-start(bf16[2,2,1280,128]{3,2,1,0:T(8,128)(2,1)} %keys.1) | copy-start | bytes 3932164
  35.1 1.3 %copy-start.3 = (bf16[2,2,1280,128]{3,2,1,0:T(8,128)(2,1)S(1)}, bf16[2,2,1280,128]{3,2,1,0:T(8,128)(2,1)}, u32[]{:S(2)}) copy-start(bf16[2,2,1280,128]{3,2,1,0:T(8,128)(2,1)} %values.1) | copy-start | bytes 3932164
  36.4 0.7 copy-start.5
  45.9 27.7 %all-to-all-start.1 = ((bf16[8,2,16,1920]{3,2,1,0:T(8,128)(2,1)}), bf16[8,2,16,1920]{3,2,1,0:T(8,128)(2,1)S(1)}, u32[]{:S(2)}, u32[]{:S(2)}) async-start(bf16[8,2,16,1920]{3,2,1,0:T(8,128)(2,1)} %image_attention.1), calls=%async_computation.1 | async-start | bytes 1966080 | tf_op jit(solution)/shard_map/all_to_all | solution.py:208

commit v3 on v2

--- a/solution.py
+++ b/solution.py
@@ -93,7 +93,7 @@
         ],
         out_specs=pl.BlockSpec((lead, None, inner, wide), lambda i: (0, i, 0, 0)),
         out_shape=jax.ShapeDtypeStruct((lead, held, inner, wide), jnp.bfloat16),
-        compiler_params=pltpu.CompilerParams(vmem_limit_bytes=48 * 1024 * 1024),
+        compiler_params=pltpu.CompilerParams(vmem_limit_bytes=32 * 1024 * 1024),
         name="image_attention",
     )(image_lengths, incoming, image_keys, image_values)
     if count % 16:
@@ -103,28 +103,27 @@
 
 def prepare_body(request_image, image_slot, queries, outgoing, targets, *, most):
     local_heads, rows, _ = queries.shape
-    images = image_slot.shape[1]
-    ids = lax.broadcasted_iota(jnp.int32, (rows, images), 1)
-    slot_values = jnp.where(request_image[...] == ids, image_slot[...], 0).astype(jnp.float32)
-    slots = jnp.sum(slot_values, axis=1, keepdims=True)
-    hits = jnp.where(ids.astype(jnp.float32) == slots, 1.0, 0.0)
-    earlier = lax.broadcasted_iota(jnp.int32, (rows, rows), 1) < lax.broadcasted_iota(
-        jnp.int32, (rows, rows), 0
+    images = image_slot.shape[0]
+    chosen = request_image[...]
+    slots = jnp.zeros((1, rows), jnp.int32)
+    for image in range(images):
+        slots = jnp.where(chosen == image, image_slot[image], slots)
+    hits = jnp.where(lax.broadcasted_iota(jnp.int32, (images, rows), 0) == slots, 1.0, 0.0)
+    earlier = lax.broadcasted_iota(jnp.int32, (rows, rows), 0) < lax.broadcasted_iota(
+        jnp.int32, (rows, rows), 1
     )
     before = jnp.dot(
+        hits.astype(jnp.bfloat16),
         jnp.where(earlier, 1.0, 0.0).astype(jnp.bfloat16),
-        hits.astype(jnp.bfloat16),
         preferred_element_type=jnp.float32,
     )
-    ranks = jnp.sum(hits * before, axis=1, keepdims=True)
-    places = (slots * most + ranks).astype(jnp.int32)
+    ranks = jnp.sum(hits * before, axis=0, keepdims=True)
+    places = slots * most + ranks.astype(jnp.int32)
     targets[...] = places
-    columns = lax.broadcasted_iota(jnp.int32, (rows, images * most), 1)
-    dispatch = jnp.where(columns == places, 1.0, 0.0).astype(jnp.bfloat16)
+    lines = lax.broadcasted_iota(jnp.int32, (images * most, rows), 0)
+    dispatch = jnp.where(lines == places, 1.0, 0.0).astype(jnp.bfloat16)
     flat = jnp.concatenate([queries[h] for h in range(local_heads)], axis=1)
-    outgoing[...] = lax.dot_general(
-        dispatch, flat, (((0,), (0,)), ((), ())), preferred_element_type=jnp.float32
-    ).astype(jnp.bfloat16)
+    outgoing[...] = jnp.dot(dispatch, flat, preferred_element_type=jnp.float32).astype(jnp.bfloat16)
 
 
 def prepare(request_image, image_slot, queries, most):
@@ -134,20 +133,26 @@
         functools.partial(prepare_body, most=most),
         out_shape=(
             jax.ShapeDtypeStruct((images * most, local_heads * head_size), jnp.bfloat16),
-            jax.ShapeDtypeStruct((rows, 1), jnp.int32),
+            jax.ShapeDtypeStruct((1, rows), jnp.int32),
         ),
+        in_specs=[
+            pl.BlockSpec(memory_space=pltpu.VMEM),
+            pl.BlockSpec(memory_space=pltpu.SMEM),
+            pl.BlockSpec(memory_space=pltpu.VMEM),
+        ],
         compiler_params=pltpu.CompilerParams(vmem_limit_bytes=16 * 1024 * 1024),
         name="prepare",
-    )(request_image, image_slot.reshape(1, images), queries.transpose(1, 0, 2))
+    )(request_image.reshape(1, rows), image_slot, queries.transpose(1, 0, 2))
 
 
 def merge_body(targets, back, text, text_lse, out):
     local_heads, rows, head_size = out.shape
     places = back.shape[0]
     width = local_heads * head_size
-    columns = lax.broadcasted_iota(jnp.int32, (rows, places), 1)
-    dispatch = jnp.where(columns == targets[...], 1.0, 0.0).astype(jnp.bfloat16)
-    pieces = jnp.dot(dispatch, back[:, width:], preferred_element_type=jnp.float32)
+    lines = lax.broadcasted_iota(jnp.int32, (places, rows), 0)
+    dispatch = jnp.where(lines == targets[...], 1.0, 0.0).astype(jnp.bfloat16)
+    across = (((0,), (0,)), ((), ()))
+    pieces = lax.dot_general(dispatch, back[:, width:], across, preferred_element_type=jnp.float32)
     source = lax.broadcasted_iota(jnp.int32, (LANES, LANES), 0)
     target = lax.broadcasted_iota(jnp.int32, (LANES, LANES), 1)
     joined = (source == target) & (target < local_heads)
@@ -161,7 +166,7 @@
     upper = jnp.maximum(image_lse, text_lse[...])
     image_weight = jnp.exp(image_lse - upper)
     share = image_weight / (image_weight + jnp.exp(text_lse[...] - upper))
-    image = jnp.dot(dispatch, back[:, :width], preferred_element_type=jnp.float32)
+    image = lax.dot_general(dispatch, back[:, :width], across, preferred_element_type=jnp.float32)
     for h in range(local_heads):
         own = text[h]
         part = image[:, h * head_size : (h + 1) * head_size]
@@ -169,7 +174,7 @@
 
 
 def merge(targets, back, text, text_lse, local_heads):
-    rows = targets.shape[0]
+    rows = targets.shape[1]
     head_size = text.shape[2]
     return pl.pallas_call(
         merge_body,
@@ -204,9 +209,6 @@
     outgoing, targets = prepare(request_image, image_slot, queries, most)
     outgoing = outgoing.reshape(devices, held, most, width)
     incoming = lax.all_to_all(outgoing, "seq", split_axis=0, concat_axis=0, tiled=True)
-    stacked = attend_images(incoming, image_keys, image_values, image_lengths, group, scale)
-    back = lax.all_to_all(stacked, "seq", split_axis=0, concat_axis=0, tiled=True)
-    flat_back = back.reshape(images * most, width + LANES)
     heads = queries.reshape(rows, local_kv, group, head_size)
     scores = (
         jnp.einsum("rhgd,rhtd->rhgt", heads, text_keys, preferred_element_type=jnp.float32) * scale
@@ -221,7 +223,12 @@
     )
     text_lse = highest[..., 0] + jnp.log(total[..., 0])
     text_flat = text_out.reshape(rows, local_heads, head_size).transpose(1, 0, 2)
-    return merge(targets, flat_back, text_flat, text_lse.reshape(rows, local_heads), local_heads)
+    text_lse = text_lse.reshape(rows, local_heads)
+    incoming, text_flat, text_lse = lax.optimization_barrier((incoming, text_flat, text_lse))
+    stacked = attend_images(incoming, image_keys, image_values, image_lengths, group, scale)
+    back = lax.all_to_all(stacked, "seq", split_axis=0, concat_axis=0, tiled=True)
+    flat_back = back.reshape(images * most, width + LANES)
+    return merge(targets, flat_back, text_flat, text_lse, local_heads)
 
 
 def solution(mesh):

time: 75.4 us -> 74.9 us (level)
  blocking collectives: 30.5 us -> 0 us
  waiting for transfers between devices: 14.4 us -> 36.6 us
  starting transfers between devices: 3.55 us -> 10.9 us
  local copies, waits for them, and re-layouts: 6.3 us -> 4.26 us
  Pallas kernels: 11.1 us -> 12.5 us
    all_to_all x1 -> x0, blocking collectives: 30.5 us -> none  [on_device(): lax.all_to_all(outgoing, 'seq', split_axis=0, concat_axis=0, tiled=True)]
    all_to_all x0 -> x1, waiting for transfers between devices: none -> 12.2 us  [on_device(): lax.all_to_all(outgoing, 'seq', split_axis=0, concat_axis=0, tiled=True)]
    all_to_all x1, waiting for transfers between devices: 14.4 us -> 24.4 us  [on_device(): lax.all_to_all(stacked, 'seq', split_axis=0, concat_axis=0, tiled=True)]
    all_to_all x0 -> x1, starting transfers between devices: none -> 7.31 us  [on_device(): lax.all_to_all(outgoing, 'seq', split_axis=0, concat_axis=0, tiled=True)]
    unnamed x15 -> x14, local copies, waits for them, and re-layouts: 5.73 us -> 3.69 us
    pallas_call x1, Pallas kernels: 0.79 us -> 2.06 us  [prepare(): pl.pallas_call(functools.partial(prepare_body, most=most), out_shape=(jax...]
  transfers between devices with their start and end apart: 1 -> 2, of which waited for: 1 -> 2; matrix products, arithmetic and copies ran while one was open for 13% -> 15% of each run, Pallas kernels for 0% -> 0%
where the time goes in v3:
time: 74.9 us; the launch traced here: 74.5 us
  waiting for transfers between devices  36.6 us (49%)
  Pallas kernels  12.5 us (17%)
  starting transfers between devices  10.9 us (15%)
  matrix products  8.68 us (12%)
  local copies, waits for them, and re-layouts  4.26 us (6%)
  other arithmetic  1.58 us (2%)
    all_to_all x1, waiting for transfers between devices, on_device(): lax.all_to_all(stacked, 'seq', split_axis=0, concat_axis=0, tiled=True)  24.4 us
    all_to_all x1, waiting for transfers between devices, on_device(): lax.all_to_all(outgoing, 'seq', split_axis=0, concat_axis=0, tiled=True)  12.2 us
    pallas_call x1, Pallas kernels, attend_images(): pl.pallas_call(functools.partial(image_body, group=group, scale=scale), g...  8.92 us
    all_to_all x1, starting transfers between devices, on_device(): lax.all_to_all(outgoing, 'seq', split_axis=0, concat_axis=0, tiled=True)  7.31 us
    dot_general x1, matrix products, on_device(): jnp.einsum('rhgd,rhtd->rhgt', heads, text_keys, preferred_element_type=jn...  4.78 us
    dot_general x1, matrix products, on_device(): jnp.einsum('rhgt,rhtd->rhgd', weights, text_values, preferred_element_typ...  3.9 us
    unnamed x14, local copies, waits for them, and re-layouts  3.69 us
    all_to_all x1, starting transfers between devices, on_device(): lax.all_to_all(stacked, 'seq', split_axis=0, concat_axis=0, tiled=True)  3.55 us
  transfers between devices with their start and end apart: 2, of which 2 were waited for; matrix products, arithmetic and copies ran while one was open for 15% of the time, Pallas kernels for 0%

profile of v3, /device:TPU:0, one launch (start us, length us, event | category | flops | bytes accessed | tf_op | source)
XLA Modules:
  0.0 74.5 jit_solution(9217447179247024023)
XLA Ops:
  0.0 0.0 copy-start
  0.0 1.0 %copy-done = bf16[128,14,128]{2,0,1:T(8,128)(2,1)S(1)} copy-done((bf16[128,14,128]{2,0,1:T(8,128)(2,1)S(1)}, bf16[128,14,128]{2,0,1:T(8,128)(2,1)}, u32[]{:S(2)}) %copy-start) | copy-done | bytes 458776
  1.0 0.0 copy-start.3
  1.0 0.7 copy-done.3
  1.7 0.0 copy-start.4
  1.7 0.7 copy-done.4
  2.3 2.1 %prepare.1 = (bf16[256,1792]{1,0:T(8,128)(2,1)}, s32[1,128]{1,0:T(1,128)S(1)}) custom-call(s32[1,128]{1,0:T(1,128)S(1)} %bitcast.17, s32[16]{0:T(128)S(1)} %copy-done.4, bf16[14,128,128]{2,1,0:T(8,128)(2,1)S(1)} %bitcast.16), custom_call_target="tpu_custom_call" | custom-call | tf_op jit(solution)/shard_map/prepare/pallas_call | solution.py:132
  4.4 7.3 %all-to-all-start = ((bf16[8,2,16,1792]{3,2,1,0:T(8,128)(2,1)}), bf16[8,2,16,1792]{3,2,1,0:T(8,128)(2,1)S(1)}, u32[]{:S(2)}, u32[]{:S(2)}) async-start(bf16[8,2,16,1792]{3,2,1,0:T(8,128)(2,1)} %bitcast.2), calls=%async_computation | async-start | bytes 1835008 | tf_op jit(solution)/shard_map/all_to_all | solution.py:211
  11.7 0.7 iota_compare_fusion
  12.4 4.8 %fusion.9 = (f32[128,2,7]{2,1,0:T(2,128)S(1)}, f32[128,2,7,64]{3,2,1,0:T(8,128)S(1)}) fusion(bf16[128,2,64,128]{3,2,1,0:T(8,128)(2,1)} %param.15, bf16[128,2,7,128]{3,0,2,1:T(8,128)(2,1)} %bitcast.15, pred[128,64]{1,0:T(8,128)(4,1)S(1)} %iota_compare_fusion), kind=kOutput, calls=%fused_computation.13 | convolution fusion | flops 29702400 | bytes 5127168 | tf_op jit(solution)/shard_map/rhgd,rhtd->rhgt/dot_general | solution.py:214
  17.2 0.0 copy-start.6
  17.2 0.1 copy.24
  17.3 0.8 %fusion.1 = f32[128,2,7]{2,1,0:T(2,128)S(1)} fusion(f32[128,2,7,64]{3,2,1,0:T(8,128)S(1)} %get-tuple-element.16, f32[128,2,7]{2,1,0:T(2,128)S(1)} %get-tuple-element.15, pred[128,64]{1,0:T(8,128)(4,1)S(1)} %iota_compare_fusion), kind=kLoop, calls=%fused_computation.4 | loop fusion | flops 342272 | bytes 481280 | tf_op jit(solution)/shard_map/reduce_sum | solution.py:18
  18.2 0.0 copy-done.6
  18.2 0.1 copy.23
  18.3 0.0 copy-start.1
  18.3 0.0 copy-start.5
  18.3 3.9 %convolution_divide_fusion = f32[128,2,7,128]{3,2,1,0:T(8,128)S(1)} fusion(bf16[128,2,64,128]{3,2,1,0:T(8,128)(2,1)} %param.16, f32[128,2,7,64]{3,2,1,0:T(8,128)} %copy-done.6, f32[128,2,7]{2,1,0:T(2,128)S(1)} %fusion.1, f32[128,2,7]{2,1,0:T(2,128)S(1)} %get-tuple-element.15, pred[128,64]{1,0:T(8,128)(4,1)S(1)} %iota_compare_fusion), kind=kOutput, calls=%fused_computation | convolution fusion | flops 29933568 | bytes 5593088 | tf_op jit(solution)/shard_map/rhgt,rhtd->rhgd/dot_general | solution.py:221
  22.2 0.3 copy.22
  22.5 12.2 %all-to-all-done.queries = bf16[8,2,16,1792]{3,2,1,0:T(8,128)(2,1)S(1)} async-done(((bf16[8,2,16,1792]{3,2,1,0:T(8,128)(2,1)}), bf16[8,2,16,1792]{3,2,1,0:T(8,128)(2,1)S(1)}, u32[]{:S(2)}, u32[]{:S(2)}) %all-to-all-start) | async-done | bytes 917536 | tf_op jit(solution)/shard_map/all_to_all | solution.py:211
  34.7 0.0 copy-done.1
  34.7 0.0 copy-done.5
  34.7 0.0 copy-start.2
  34.7 1.3 %copy-done.2 = bf16[2,2,1280,128]{3,2,1,0:T(8,128)(2,1)S(1)} copy-done((bf16[2,2,1280,128]{3,2,1,0:T(8,128)(2,1)S(1)}, bf16[2,2,1280,128]{3,2,1,0:T(8,128)(2,1)}, u32[]{:S(2)}) %copy-start.2) | copy-done | bytes 1310744
  36.1 8.9 %image_attention.1 = bf16[8,2,16,1920]{3,2,1,0:T(8,128)(2,1)} custom-call(s32[2]{0:T(128)S(1)} %copy-done.5, bf16[8,2,16,1792]{3,2,1,0:T(8,128)(2,1)S(1)} %all-to-all-done.queries, bf16[2,2,1280,128]{3,2,1,0:T(8,128)(2,1)S(1)} %copy-done.1, bf16[2,2,1280,128]{3,2,1,0:T(8,128)(2,1)S(1)} %copy-done.2), custom_call_target="tpu_custom_call" | custom-call | tf_op jit(solution)/shard_map/image_attention/pallas_call | solution.py:85
  45.0 3.6 %all-to-all-start.1 = ((bf16[8,2,16,1920]{3,2,1,0:T(8,128)(2,1)}), bf16[8,2,16,1920]{3,2,1,0:T(8,128)(2,1)S(1)}, u32[]{:S(2)}, u32[]{:S(2)}) async-start(bf16[8,2,16,1920]{3,2,1,0:T(8,128)(2,1)} %image_attention.1), calls=%async_computation.1 | async-start | bytes 1966080 | tf_op jit(solution)/shard_map/all_to_all | solution.py:229
  48.5 0.1 copy.26.text_lse
  48.6 24.4 %all-to-all-done.1 = bf16[8,2,16,1920]{3,2,1,0:T(8,128)(2,1)S(1)} async-done(((bf16[8,2,16,1920]{3,2,1,0:T(8,128)(2,1)}), bf16[8,2,16,1920]{3,2,1,0:T(8,128)(2,1)S(1)}, u32[]{:S(2)}, u32[]{:S(2)}) %all-to-all-start.1) | async-done | bytes 983072 | tf_op jit(solution)/shard_map/all_to_all | solution.py:229
  73.0 1.5 %merge.1 = bf16[14,128,128]{2,1,0:T(8,128)(2,1)} custom-call(s32[1,128]{1,0:T(1,128)S(1)} %get-tuple-element.10.targets, bf16[256,1920]{1,0:T(8,128)(2,1)S(1)} %bitcast.13, f32[14,128,128]{2,1,0:T(8,128)S(1)} %bitcast.14, f32[128,14]{1,0:T(8,128)S(1)} %copy.26.text_lse), custom_call_target="tpu_custom_call" | custom-call | tf_op jit(solution)/shard_map/merge/pallas_call | solution.py:179
  (3 shorter events, 0.0 us)
Async XLA Ops:
  0.0 1.0 %copy-start = (bf16[128,14,128]{2,0,1:T(8,128)(2,1)S(1)}, bf16[128,14,128]{2,0,1:T(8,128)(2,1)}, u32[]{:S(2)}) copy-start(bf16[128,14,128]{2,0,1:T(8,128)(2,1)} %param.9) | copy-start | bytes 1376260
  1.0 0.7 copy-start.3
  1.7 0.7 copy-start.4
  4.4 30.3 %all-to-all-start = ((bf16[8,2,16,1792]{3,2,1,0:T(8,128)(2,1)}), bf16[8,2,16,1792]{3,2,1,0:T(8,128)(2,1)S(1)}, u32[]{:S(2)}, u32[]{:S(2)}) async-start(bf16[8,2,16,1792]{3,2,1,0:T(8,128)(2,1)} %bitcast.2), calls=%async_computation | async-start | bytes 1835008 | tf_op jit(solution)/shard_map/all_to_all | solution.py:211
  17.2 1.0 %copy-start.6 = (f32[128,2,7,64]{3,2,1,0:T(8,128)}, f32[128,2,7,64]{3,2,1,0:T(8,128)S(1)}, u32[]{:S(2)}) copy-start(f32[128,2,7,64]{3,2,1,0:T(8,128)S(1)} %get-tuple-element.16) | copy-start | bytes 1376260
  18.3 16.4 %copy-start.1 = (bf16[2,2,1280,128]{3,2,1,0:T(8,128)(2,1)S(1)}, bf16[2,2,1280,128]{3,2,1,0:T(8,128)(2,1)}, u32[]{:S(2)}) copy-start(bf16[2,2,1280,128]{3,2,1,0:T(8,128)(2,1)} %keys.1) | copy-start | bytes 3932164
  18.3 16.4 %copy-start.5 = (s32[2]{0:T(128)S(1)}, s32[2]{0:T(128)}, u32[]{:S(2)}) copy-start(s32[2]{0:T(128)} %lengths.1) | copy-start | bytes 28
  34.7 1.3 %copy-start.2 = (bf16[2,2,1280,128]{3,2,1,0:T(8,128)(2,1)S(1)}, bf16[2,2,1280,128]{3,2,1,0:T(8,128)(2,1)}, u32[]{:S(2)}) copy-start(bf16[2,2,1280,128]{3,2,1,0:T(8,128)(2,1)} %values.1) | copy-start | bytes 3932164
  45.0 28.1 %all-to-all-start.1 = ((bf16[8,2,16,1920]{3,2,1,0:T(8,128)(2,1)}), bf16[8,2,16,1920]{3,2,1,0:T(8,128)(2,1)S(1)}, u32[]{:S(2)}, u32[]{:S(2)}) async-start(bf16[8,2,16,1920]{3,2,1,0:T(8,128)(2,1)} %image_attention.1), calls=%async_computation.1 | async-start | bytes 1966080 | tf_op jit(solution)/shard_map/all_to_all | solution.py:229
